TPU v7x, 32 devices: a whole 2x2x4 slice. The times are simulated.
32 devices in a mesh: space: 8 (over z, y), tm: 4 (over x, core).
Axes of the slice: x: 2, y: 2, z: 4, core: 2. Of those that a mesh axis runs over, the one named last changes fastest.
Arguments:
- precip: float32 [512, 48, 2048], P('tm', 'space'), may hold values from 0.0001 to 0.01
Outputs:
- totals: float32 [48, 2048, 512], P(None, 'space', 'tm')
All inputs are finite; a program needn't handle non-finite values.
Results may differ from a plain program's by a relative error of at most 0.00005.
Values sent between devices are 32-bit elements; how exact they have to be, the bound alone decides.
A program may use at most 64 MiB of HBM per device.

v0:
```python
import functools

import jax
import jax.numpy as jnp
from jax import lax
from jax.experimental import pallas as pl
from jax.experimental.pallas import tpu as pltpu
from jax.sharding import PartitionSpec as P

MESH = pl.DeviceIdType.MESH
HEAD = 8
CHUNKS = 2
FIRST = 3


def turns_of(spaces):
    near = list(range(1, spaces))
    if spaces & (spaces - 1) or spaces < 4:
        return near, near
    return near, [step ^ 1 for step in near[1:]] + [1]


def flip(place, mask, size):
    value, bit = 0, 1
    while bit < size:
        value = value + ((place // bit + mask // bit) % 2) * bit
        bit *= 2
    return value


def peer_at(place, step, size):
    if size & (size - 1) == 0:
        return flip(place, step, size)
    return lax.rem(place + step, size)


def source_at(place, step, size):
    if size & (size - 1) == 0:
        return flip(place, step, size)
    return lax.rem(place + size - step, size)


def kernel(spaces, times, chunks, x_ref, out_ref, held, arrived, tot, tots, ones,
           load_sem, main_send, main_recv, head_send, head_recv, tot_send, tot_recv):
    lat, days, lon = x_ref.shape
    block = lon // spaces
    part = lat // chunks
    me = lax.axis_index("space")
    when = lax.axis_index("tm")

    loads = [pltpu.make_async_copy(x_ref.at[a], held.at[a], load_sem.at[a]) for a in range(lat)]
    barrier = pltpu.get_barrier_semaphore()
    for step in range(1, spaces):
        pl.semaphore_signal(barrier, inc=1, device_id={"space": peer_at(me, step, spaces)}, device_id_type=MESH)
    for step in range(1, times):
        pl.semaphore_signal(barrier, inc=1, device_id={"tm": lax.rem(when + step, times)}, device_id_type=MESH)
    for load in loads:
        load.start()
    pl.semaphore_wait(barrier, spaces - 1 + times - 1)

    def columns(step):
        peer = peer_at(me, step, spaces)
        return peer, pl.ds(pl.multiple_of(peer * block, block), block)

    def main(step, c):
        peer, cols = columns(step)
        return pltpu.make_async_remote_copy(
            src_ref=x_ref.at[pl.ds(c * part, part), pl.ds(HEAD, days - HEAD), cols],
            dst_ref=arrived.at[step - 1, pl.ds(c * part, part), pl.ds(HEAD, days - HEAD)],
            send_sem=main_send.at[step - 1, c],
            recv_sem=main_recv.at[step - 1, c],
            device_id={"space": peer},
            device_id_type=MESH,
        )

    def head(step):
        peer, cols = columns(step)
        return pltpu.make_async_remote_copy(
            src_ref=held.at[:, pl.ds(0, HEAD), cols],
            dst_ref=arrived.at[step - 1, :, pl.ds(0, HEAD)],
            send_sem=head_send.at[step - 1],
            recv_sem=head_recv.at[step - 1],
            device_id={"space": peer},
            device_id_type=MESH,
        )

    def total(step):
        return pltpu.make_async_remote_copy(
            src_ref=tot,
            dst_ref=tots.at[step - 1],
            send_sem=tot_send.at[step - 1],
            recv_sem=tot_recv.at[step - 1],
            device_id={"tm": lax.rem(when + step, times)},
            device_id_type=MESH,
        )

    first = min(FIRST, spaces - 1)
    even, odd = turns_of(spaces)
    turns = [a if a == b else jnp.where(when % 2 == 0, a, b) for a, b in zip(even, odd)]
    for step in turns[:first]:
        for c in range(chunks):
            main(step, c).start()

    for a in range(lat):
        loads[a].wait()
        tot[a] = jnp.sum(held[a], axis=0, keepdims=True)
    position = lax.broadcasted_iota(jnp.int32, (days, days), 0)
    later = lax.broadcasted_iota(jnp.int32, (days, days), 1)
    ones[...] = (position <= later).astype(jnp.float32)
    for step in range(1, times):
        total(step).start()
    for step in range(1, times):
        total(step).wait_recv()
    for a in range(lat):
        carry = jnp.zeros((1, lon), jnp.float32)
        for step in range(1, times):
            earlier = jnp.where(when >= step, 1.0, 0.0)
            carry = carry + tots[step - 1, a] * earlier
        held[a, 0:1, :] = held[a, 0:1, :] + carry

    def prefix(x):
        return lax.dot_general(
            x.T, ones[...], (((1,), (0,)), ((), ())),
            precision=lax.Precision.HIGHEST, preferred_element_type=jnp.float32,
        )

    for step in turns:
        head(step).start()
    for step in turns[first:]:
        for c in range(chunks):
            main(step, c).start()

    mine = pl.ds(pl.multiple_of(me * block, block), block)

    @pl.loop(0, lat)
    def _(a):
        out_ref[me * lat + a] = prefix(held[a, :, mine])

    for step in turns:
        source = source_at(me, step, spaces)
        head(step).wait_recv()
        for c in range(chunks):
            main(step, c).wait_recv()

            @pl.loop(c * part, (c + 1) * part)
            def _(a):
                out_ref[source * lat + a] = prefix(arrived[step - 1, a])

    for step in range(1, times):
        total(step).wait_send()
    for step in range(1, spaces):
        head(step).wait_send()
        for c in range(chunks):
            main(step, c).wait_send()


def direct(spaces, times, precip):
    days, lat, lon = precip.shape
    chunks = CHUNKS if lat % CHUNKS == 0 else 1
    block = lon // spaces
    rows = jnp.transpose(precip, (1, 0, 2))
    dma = pltpu.SemaphoreType.DMA
    return pl.pallas_call(
        functools.partial(kernel, spaces, times, chunks),
        out_shape=jax.ShapeDtypeStruct((lat * spaces, block, days), jnp.float32),
        in_specs=[pl.BlockSpec(memory_space=pltpu.HBM)],
        out_specs=pl.BlockSpec(memory_space=pltpu.VMEM),
        scratch_shapes=[
            pltpu.VMEM((lat, days, lon), jnp.float32),
            pltpu.VMEM((spaces - 1, lat, days, block), jnp.float32),
            pltpu.VMEM((lat, 1, lon), jnp.float32),
            pltpu.VMEM((times - 1, lat, 1, lon), jnp.float32),
            pltpu.VMEM((days, days), jnp.float32),
            dma((lat,)),
            dma((spaces - 1, chunks)),
            dma((spaces - 1, chunks)),
            dma((spaces - 1,)),
            dma((spaces - 1,)),
            dma((times - 1,)),
            dma((times - 1,)),
        ],
        compiler_params=pltpu.CompilerParams(
            collective_id=0, has_side_effects=True, vmem_limit_bytes=46 * 2**20
        ),
        name="rechunk",
    )(rows)


def plain(precip):
    days = precip.shape[0]
    position = lax.broadcasted_iota(jnp.int32, (days, days), 0)
    later = lax.broadcasted_iota(jnp.int32, (days, days), 1)
    ones = (position <= later).astype(jnp.float32)
    source = lax.all_to_all(precip, "space", split_axis=2, concat_axis=1, tiled=True)
    pixel_major = jnp.transpose(source, (1, 2, 0))
    running = jnp.dot(
        pixel_major, ones, precision=lax.Precision.HIGHEST, preferred_element_type=jnp.float32
    )
    last = lax.all_gather(running[:, :, -1], "tm")
    place = lax.broadcasted_iota(jnp.int32, last.shape, 0)
    carried = jnp.sum(jnp.where(place < lax.axis_index("tm"), last, 0.0), axis=0)
    return running + carried[:, :, None]


def solution(mesh):
    spaces, times = mesh.shape["space"], mesh.shape["tm"]

    def per_device(precip):
        days, _, lon = precip.shape
        tiled = lon % (spaces * 128) == 0 and days % 128 == 0
        if tiled and spaces > 1 and times > 1:
            return direct(spaces, times, precip)
        return plain(precip)

    return jax.shard_map(
        per_device,
        mesh=mesh,
        in_specs=(P("tm", "space", None),),
        out_specs=P(None, "space", "tm"),
        check_vma=False,
    )
```

profile of v0, /device:TPU:8, one launch (start us, length us, event | category | flops | bytes accessed | tf_op | source)
XLA Modules:
  0.0 144.3 jit_solution(5779856882293379766)
XLA Ops:
  0.0 141.6 %rechunk.1 = f32[48,256,128]{2,1,0:T(8,128)S(1)} custom-call(f32[6,128,2048]{2,1,0:T(8,128)} %bitcast.1), custom_call_target="tpu_custom_call" | custom-call | tf_op jit(solution)/shard_map/rechunk/pallas_call | solution.py:163
  141.6 2.7 %copy.3 = f32[48,256,128]{2,1,0:T(8,128)} copy(f32[48,256,128]{2,1,0:T(8,128)S(1)} %rechunk.1) | data formatting | bytes 12582912
where the time goes:
time: 144 us
  Pallas kernels  142 us (99%)
  local copies, waits for them, and re-layouts  2.71 us (2%)
    pallas_call x1, Pallas kernels, direct(): pl.pallas_call(functools.partial(kernel, spaces, times, chunks), out_shap...  142 us

commit v1 on v0

v1 whole, which is shorter than its diff:
```python
import functools

import jax
import jax.numpy as jnp
from jax import lax
from jax.experimental import pallas as pl
from jax.experimental.pallas import tpu as pltpu
from jax.sharding import PartitionSpec as P

MESH = pl.DeviceIdType.MESH
HEAD = 8
FIRST = 4
ROW = 2
INNER = {8: ((6, 5, 1, 2, 3, 4, 7), (6, 1, 2, 3, 5, 4, 7))}
OUTER = {8: ((2, 3, 1, 7, 6, 5, 4), (2, 1, 3, 7, 6, 5, 4))}
PARTS = (3, 2, 1)


def parts_of(lat):
    total = sum(PARTS)
    if lat % total:
        return ((0, lat),)
    unit, at, found = lat // total, 0, []
    for part in PARTS:
        found.append((at, part * unit))
        at += part * unit
    return tuple(found)


def flip(place, mask, size):
    value, bit = 0, 1
    while bit < size:
        value = value + ((place // bit + mask // bit) % 2) * bit
        bit *= 2
    return value


def kernel(spaces, times, parts, x_ref, out_ref, held, arrived, tot, tots, ones,
           load_sem, main_send, main_recv, head_send, head_recv, tot_send, tot_recv, up, across, go):
    lat, days, lon = x_ref.shape
    block = lon // spaces
    rows = spaces // ROW
    low, high = rows // 2 - 1, rows // 2
    me = lax.axis_index("space")
    when = lax.axis_index("tm")
    z, y = me // ROW, me % ROW
    inner = (z == low) | (z == high)

    def pick(tables):
        return [a if a == b else jnp.where(inner, a, b) for a, b in zip(*tables)]

    sends = pick((INNER[spaces][0], OUTER[spaces][0]))
    turns = pick((INNER[spaces][1], OUTER[spaces][1]))

    def columns(place):
        return pl.ds(pl.multiple_of(place * block, block), block)

    order = [flip(me, step, spaces) for step in sends] + [me]
    pieces = len(parts)

    def load_of(place, at, size, k):
        span = pl.ds(at, size)
        return pltpu.make_async_copy(
            x_ref.at[span, :, columns(place)], held.at[span, :, columns(place)], load_sem.at[k]
        )

    loads = [load_of(order[0], at, size, k) for k, (at, size) in enumerate(parts)]
    loads += [load_of(place, 0, lat, pieces + k) for k, place in enumerate(order[1:])]

    barrier = pltpu.get_barrier_semaphore()

    def signal(semaphore, **place):
        pl.semaphore_signal(semaphore, inc=1, device_id=place, device_id_type=MESH)

    def ends(semaphore):
        for k in range(ROW):
            for j in range(times):
                if k or j:
                    signal(semaphore, space=(y + k) % ROW, tm=(when + j) % times)

    @pl.when(z < rows - 1)
    def _():
        signal(barrier, space=me + ROW)

    @pl.when((z > 0) & (z <= high))
    def _():
        signal(barrier, space=me - ROW)

    @pl.when(z == 0)
    def _():
        ends(barrier)

    for load in loads:
        load.start()
    group = ROW * times - 1
    pl.semaphore_wait(
        barrier, jnp.where(z > 0, 1, 0) + jnp.where(z <= low, 1, 0) + jnp.where(z == 0, group, 0)
    )

    def main(step, c):
        peer = flip(me, step, spaces)
        span = pl.ds(parts[c][0], parts[c][1])
        return pltpu.make_async_remote_copy(
            src_ref=held.at[span, pl.ds(HEAD, days - HEAD), columns(peer)],
            dst_ref=arrived.at[step - 1, span, pl.ds(HEAD, days - HEAD)],
            send_sem=main_send.at[step - 1, c],
            recv_sem=main_recv.at[step - 1, c],
            device_id={"space": peer},
            device_id_type=MESH,
        )

    def head(step):
        peer = flip(me, step, spaces)
        return pltpu.make_async_remote_copy(
            src_ref=held.at[:, pl.ds(0, HEAD), columns(peer)],
            dst_ref=arrived.at[step - 1, :, pl.ds(0, HEAD)],
            send_sem=head_send.at[step - 1],
            recv_sem=head_recv.at[step - 1],
            device_id={"space": peer},
            device_id_type=MESH,
        )

    def total(step):
        return pltpu.make_async_remote_copy(
            src_ref=tot,
            dst_ref=tots.at[step - 1],
            send_sem=tot_send.at[step - 1],
            recv_sem=tot_recv.at[step - 1],
            device_id={"tm": lax.rem(when + step, times)},
            device_id_type=MESH,
        )

    loads[0].wait()
    main(sends[0], 0).start()

    @pl.when(z < rows - 1)
    def _():
        pl.semaphore_wait(up, 1)

    @pl.when(z > 0)
    def _():
        signal(up, space=me - ROW)

    @pl.when(z == 0)
    def _():
        ends(across)
        pl.semaphore_wait(across, group)
        for k in range(1, rows):
            signal(go, space=me + k * ROW)

    for load in loads[1:]:
        load.wait()
    for a in range(lat):
        tot[a] = jnp.sum(held[a], axis=0, keepdims=True)
    position = lax.broadcasted_iota(jnp.int32, (days, days), 0)
    later = lax.broadcasted_iota(jnp.int32, (days, days), 1)
    ones[...] = (position <= later).astype(jnp.float32)

    @pl.when(z > 0)
    def _():
        pl.semaphore_wait(go, 1)

    for step in range(1, times):
        total(step).start()
    for step in sends[1:FIRST]:
        for c in range(pieces):
            main(step, c).start()
    for step in range(1, times):
        total(step).wait_recv()
    for a in range(lat):
        carry = jnp.zeros((1, lon), jnp.float32)
        for step in range(1, times):
            earlier = jnp.where(when >= step, 1.0, 0.0)
            carry = carry + tots[step - 1, a] * earlier
        held[a, 0:1, :] = held[a, 0:1, :] + carry

    def prefix(x):
        return lax.dot_general(
            x.T, ones[...], (((1,), (0,)), ((), ())),
            precision=lax.Precision.HIGHEST, preferred_element_type=jnp.float32,
        )

    for step in sends:
        head(step).start()
    for step in sends[FIRST:]:
        for c in range(pieces):
            main(step, c).start()
    for c in range(1, pieces):
        main(sends[0], c).start()

    @pl.loop(0, lat)
    def _(a):
        out_ref[me * lat + a] = prefix(held[a, :, columns(me)])

    def receive(step, c):
        source = flip(me, step, spaces)
        main(step, c).wait_recv()

        @pl.loop(parts[c][0], parts[c][0] + parts[c][1])
        def _(a):
            out_ref[source * lat + a] = prefix(arrived[step - 1, a])

    head(turns[0]).wait_recv()
    receive(turns[0], 0)
    for step in turns[1:]:
        head(step).wait_recv()
        for c in range(pieces):
            receive(step, c)

    for step in range(1, times):
        total(step).wait_send()
    for step in sends:
        head(step).wait_send()
        for c in range(pieces if step is not sends[0] else 1):
            main(step, c).wait_send()
    for c in range(1, pieces):
        receive(turns[0], c)
    for c in range(1, pieces):
        main(sends[0], c).wait_send()


def direct(spaces, times, precip):
    days, lat, lon = precip.shape
    parts = parts_of(lat)
    pieces = len(parts)
    block = lon // spaces
    rows = jnp.transpose(precip, (1, 0, 2))
    dma, plain_sem = pltpu.SemaphoreType.DMA, pltpu.SemaphoreType.REGULAR
    return pl.pallas_call(
        functools.partial(kernel, spaces, times, parts),
        out_shape=jax.ShapeDtypeStruct((lat * spaces, block, days), jnp.float32),
        in_specs=[pl.BlockSpec(memory_space=pltpu.HBM)],
        out_specs=pl.BlockSpec(memory_space=pltpu.VMEM),
        scratch_shapes=[
            pltpu.VMEM((lat, days, lon), jnp.float32),
            pltpu.VMEM((spaces - 1, lat, days, block), jnp.float32),
            pltpu.VMEM((lat, 1, lon), jnp.float32),
            pltpu.VMEM((times - 1, lat, 1, lon), jnp.float32),
            pltpu.VMEM((days, days), jnp.float32),
            dma((pieces + spaces - 1,)),
            dma((spaces - 1, pieces)),
            dma((spaces - 1, pieces)),
            dma((spaces - 1,)),
            dma((spaces - 1,)),
            dma((times - 1,)),
            dma((times - 1,)),
            plain_sem,
            plain_sem,
            plain_sem,
        ],
        compiler_params=pltpu.CompilerParams(
            collective_id=0, has_side_effects=True, vmem_limit_bytes=46 * 2**20
        ),
        name="rechunk",
    )(rows)


def plain(precip):
    days = precip.shape[0]
    position = lax.broadcasted_iota(jnp.int32, (days, days), 0)
    later = lax.broadcasted_iota(jnp.int32, (days, days), 1)
    ones = (position <= later).astype(jnp.float32)
    source = lax.all_to_all(precip, "space", split_axis=2, concat_axis=1, tiled=True)
    pixel_major = jnp.transpose(source, (1, 2, 0))
    running = jnp.dot(
        pixel_major, ones, precision=lax.Precision.HIGHEST, preferred_element_type=jnp.float32
    )
    last = lax.all_gather(running[:, :, -1], "tm")
    place = lax.broadcasted_iota(jnp.int32, last.shape, 0)
    carried = jnp.sum(jnp.where(place < lax.axis_index("tm"), last, 0.0), axis=0)
    return running + carried[:, :, None]


def solution(mesh):
    spaces, times = mesh.shape["space"], mesh.shape["tm"]

    def per_device(precip):
        days, _, lon = precip.shape
        tiled = lon % (spaces * 128) == 0 and days % 128 == 0
        if tiled and spaces in INNER and times > 1:
            return direct(spaces, times, precip)
        return plain(precip)

    return jax.shard_map(
        per_device,
        mesh=mesh,
        in_specs=(P("tm", "space", None),),
        out_specs=P(None, "space", "tm"),
        check_vma=False,
    )
```

time: 144 us -> 142 us (0.986)
  the two profiles are of different devices: /device:TPU:8 before, /device:TPU:9 now
where the time goes in v1:
time: 142 us
  Pallas kernels  139 us (98%)
  local copies, waits for them, and re-layouts  2.71 us (2%)
    pallas_call x1, Pallas kernels, direct(): pl.pallas_call(functools.partial(kernel, spaces, times, parts), out_shape...  139 us

profile of v1, /device:TPU:9, one launch (start us, length us, event | category | flops | bytes accessed | tf_op | source)
XLA Modules:
  0.0 141.7 jit_solution(8176704140496795826)
XLA Ops:
  0.0 139.0 %rechunk.1 = f32[48,256,128]{2,1,0:T(8,128)S(1)} custom-call(f32[6,128,2048]{2,1,0:T(8,128)} %bitcast.1), custom_call_target="tpu_custom_call" | custom-call | tf_op jit(solution)/shard_map/rechunk/pallas_call | solution.py:229
  139.0 2.7 %copy.3 = f32[48,256,128]{2,1,0:T(8,128)} copy(f32[48,256,128]{2,1,0:T(8,128)S(1)} %rechunk.1) | data formatting | bytes 12582912

commit v2 on v1

v2 whole, which is shorter than its diff:
```python
import functools

import jax
import jax.numpy as jnp
from jax import lax
from jax.experimental import pallas as pl
from jax.experimental.pallas import tpu as pltpu
from jax.sharding import PartitionSpec as P

MESH = pl.DeviceIdType.MESH
HEAD = 8
ROW = 2
SPLIT, LAST = 6, 7
STEPS = {
    (True, 0): ((), (5, 4, 2, 3), (), (1,), (2, 3, 1, 5, 4)),
    (True, 1): ((), (2, 3), (), (5, 4, 1), (2, 3, 1, 5, 4)),
    (False, 0): ((2,), (3,), (1, 5, 4, 7, 6), (), (2, 3, 5, 4, 1, 7, 6)),
    (False, 1): ((2,), (3,), (1, 7, 6, 5, 4), (), (2, 3, 1, 5, 4, 7, 6)),
}
SPACES = 8
PARTS = (3, 2, 1)
GRANT = 44 * 2**20


def parts_of(lat):
    total = sum(PARTS)
    if lat % total:
        return ((0, lat),)
    unit, at, found = lat // total, 0, []
    for part in PARTS:
        found.append((at, part * unit))
        at += part * unit
    return tuple(found)


def flip(place, mask, size):
    value, bit = 0, 1
    while bit < size:
        value = value + ((place // bit + mask // bit) % 2) * bit
        bit *= 2
    return value


def prefix(x, ones):
    return lax.dot_general(
        x.T, ones[...], (((1,), (0,)), ((), ())),
        precision=lax.Precision.HIGHEST, preferred_element_type=jnp.float32,
    )


def upper(ones):
    position = lax.broadcasted_iota(jnp.int32, ones.shape, 0)
    later = lax.broadcasted_iota(jnp.int32, ones.shape, 1)
    ones[...] = (position <= later).astype(jnp.float32)


def by_kind(inner, when, act):
    for (within, core) in STEPS:
        side = inner if within else jnp.logical_not(inner)
        pl.when(side & (when % 2 == core))(functools.partial(act, within, core))


def most(spaces, times, early, x_ref, out_ref, kept, held, arrived, tot, tots, ones,
         load_sem, sent, main_recv, piece_sent, piece_recv, head_recv, tot_send, tot_recv, up, across, go):
    lat, days, lon = x_ref.shape
    block = lon // spaces
    rows = spaces // ROW
    low, high = rows // 2 - 1, rows // 2
    me = lax.axis_index("space")
    when = lax.axis_index("tm")
    z, y = me // ROW, me % ROW
    inner = (z == low) | (z == high)

    def columns(place):
        return pl.ds(pl.multiple_of(place * block, block), block)

    order = [SPLIT, *(k for k in range(1, spaces) if k != SPLIT)]
    order = [flip(me, step, spaces) for step in order] + [me]

    def load_of(place, at, size, k):
        span = pl.ds(at, size)
        return pltpu.make_async_copy(
            x_ref.at[span, :, columns(place)], held.at[span, :, columns(place)], load_sem.at[k]
        )

    loads = [load_of(order[0], 0, early, 0), load_of(order[0], early, lat - early, 1)]
    loads += [load_of(place, 0, lat, 2) for place in order[1:]]

    barrier = pltpu.get_barrier_semaphore()

    def signal(semaphore, **place):
        pl.semaphore_signal(semaphore, inc=1, device_id=place, device_id_type=MESH)

    def ends(semaphore):
        for k in range(ROW):
            for j in range(times):
                if k or j:
                    signal(semaphore, space=(y + k) % ROW, tm=(when + j) % times)

    @pl.when(z < rows - 1)
    def _():
        signal(barrier, space=me + ROW)

    @pl.when((z > 0) & (z <= high))
    def _():
        signal(barrier, space=me - ROW)

    @pl.when(z == 0)
    def _():
        ends(barrier)

    for load in loads:
        load.start()
    group = ROW * times - 1
    pl.semaphore_wait(
        barrier, jnp.where(z > 0, 1, 0) + jnp.where(z <= low, 1, 0) + jnp.where(z == 0, group, 0)
    )

    def block_copy(step, at_day, size, rows_in, send_sem, recv_sem):
        peer = flip(me, step, spaces)
        span, time = pl.ds(0, rows_in), pl.ds(at_day, size)
        return pltpu.make_async_remote_copy(
            src_ref=held.at[span, time, columns(peer)],
            dst_ref=arrived.at[step - 1, span, time],
            send_sem=send_sem,
            recv_sem=recv_sem,
            device_id={"space": peer},
            device_id_type=MESH,
        )

    def main(step):
        return block_copy(step, HEAD, days - HEAD, lat, sent, main_recv.at[step - 1])

    def head(step):
        return block_copy(step, 0, HEAD, lat, sent, head_recv.at[step - 1])

    def piece():
        return block_copy(SPLIT, HEAD, days - HEAD, early, piece_sent, piece_recv.at[0])

    def piece_head():
        return block_copy(SPLIT, 0, HEAD, early, piece_sent, piece_recv.at[1])

    def total(step):
        return pltpu.make_async_remote_copy(
            src_ref=tot,
            dst_ref=tots.at[step - 1],
            send_sem=tot_send,
            recv_sem=tot_recv.at[step - 1],
            device_id={"tm": lax.rem(when + step, times)},
            device_id_type=MESH,
        )

    def send(k):
        def act(within, core):
            for step in STEPS[within, core][k]:
                main(step).start()

        by_kind(inner, when, act)

    loads[0].wait()

    @pl.when(inner)
    def _():
        piece().start()

    @pl.when(z < rows - 1)
    def _():
        pl.semaphore_wait(up, 1)

    @pl.when(z > 0)
    def _():
        signal(up, space=me - ROW)

    @pl.when(z == 0)
    def _():
        ends(across)
        pl.semaphore_wait(across, group)
        for k in range(1, rows):
            signal(go, space=me + k * ROW)

    loads[1].wait()
    pltpu.make_async_copy(arrived, arrived, load_sem.at[2]).wait()
    send(0)
    for a in range(lat):
        tot[a] = jnp.sum(held[a], axis=0, keepdims=True)
    upper(ones)

    @pl.when(z > 0)
    def _():
        pl.semaphore_wait(go, 1)

    for step in range(1, times):
        total(step).start()
    send(1)
    for step in range(1, times):
        total(step).wait_recv()
    for a in range(lat):
        carry = jnp.zeros((1, lon), jnp.float32)
        for step in range(1, times):
            earlier = jnp.where(when >= step, 1.0, 0.0)
            carry = carry + tots[step - 1, a] * earlier
        held[a, 0:1, :] = held[a, 0:1, :] + carry

    def heads(within, core):
        if within:
            piece_head().start()
        for batch in STEPS[within, core][:4]:
            for step in batch:
                head(step).start()

    by_kind(inner, when, heads)
    send(2)
    for k, step in enumerate((LAST, SPLIT)):
        place = columns(flip(me, step, spaces))

        @pl.loop(0, lat)
        def _(a):
            kept[k, a] = held[a, :, place]

    def put(source, k, rows_in):
        @pl.loop(0, rows_in)
        def _(a):
            out_ref[source * lat + a] = prefix(arrived[k, a], ones)

    @pl.loop(0, lat)
    def _(a):
        out_ref[me * lat + a] = prefix(held[a, :, columns(me)], ones)

    def arrivals(within, core):
        steps = STEPS[within, core][4]
        if within:
            main(steps[0]).wait_recv()
            for step in STEPS[within, core][3]:
                main(step).start()
            piece_head().wait_recv()
            piece().wait_recv()
            put(flip(me, SPLIT, spaces), SPLIT - 1, early)
        for step in steps:
            head(step).wait_recv()
            if not within or step != steps[0]:
                main(step).wait_recv()
            put(flip(me, step, spaces), step - 1, lat)
        count = sum(len(batch) for batch in STEPS[within, core][:4])
        blocks = arrived.at[pl.ds(0, count)]
        pltpu.make_async_copy(blocks, blocks, sent).wait()
        if within:
            rows_out = arrived.at[0, pl.ds(0, early)]
            pltpu.make_async_copy(rows_out, rows_out, piece_sent).wait()

    by_kind(inner, when, arrivals)
    pltpu.make_async_copy(tots, tots, tot_send).wait()


def put_away(first_ref, out_ref, token_ref, sem):
    copy = pltpu.make_async_copy(first_ref, out_ref, sem)
    copy.start()
    token_ref[...] = jnp.zeros_like(token_ref)
    copy.wait()


def rest(spaces, lat, parts, token_ref, kept, out_ref, got, ones, sent, received):
    days, block = got.shape[1:]
    me = lax.axis_index("space")
    z = me // ROW
    inner = (z == spaces // ROW // 2 - 1) | (z == spaces // ROW // 2)
    barrier = pltpu.get_barrier_semaphore()

    @pl.when(inner)
    def _():
        for step in (LAST, SPLIT):
            pl.semaphore_signal(
                barrier, inc=1, device_id={"space": flip(me, step, spaces)}, device_id_type=MESH
            )
        upper(ones)
        pl.semaphore_wait(barrier, 2)

    def copy(step, at, size, to, send_sem, recv_sem):
        peer = flip(me, step, spaces)
        return pltpu.make_async_remote_copy(
            src_ref=kept.at[(LAST, SPLIT).index(step), pl.ds(at, size)],
            dst_ref=got.at[pl.ds(to, size)],
            send_sem=send_sem,
            recv_sem=recv_sem,
            device_id={"space": peer},
            device_id_type=MESH,
        )

    whole = copy(LAST, 0, lat, 0, sent.at[0], received.at[0])
    at, pieces = lat, []
    for k, (start, size) in enumerate(parts[1:]):
        pieces.append((at, size, copy(SPLIT, start, size, at, sent.at[1 + k], received.at[1 + k])))
        at += size

    def put(at, size):
        @pl.loop(at, at + size)
        def _(a):
            out_ref[a] = prefix(got[a], ones)

    @pl.when(inner)
    def _():
        whole.start()
        for _, _, piece in pieces:
            piece.start()
        whole.wait_recv()
        put(0, lat)
        for k, (at, size, piece) in enumerate(pieces):
            piece.wait_recv()
            put(at, size)
        whole.wait_send()
        for _, _, piece in pieces:
            piece.wait_send()


def finish(spaces, lat, parts, all_ref, late_ref, out_ref, sem):
    me = lax.axis_index("space")
    z = me // ROW
    inner = (z == spaces // ROW // 2 - 1) | (z == spaces // ROW // 2)
    start = parts[1][0]

    def copy(step, at, to, size, k):
        return pltpu.make_async_copy(
            late_ref.at[pl.ds(at, size)],
            out_ref.at[pl.ds(flip(me, step, spaces) * lat + to, size)],
            sem.at[k],
        )

    @pl.when(inner)
    def _():
        copies = [copy(LAST, 0, 0, lat, 0), copy(SPLIT, lat, start, lat - start, 1)]
        for c in copies:
            c.start()
        for c in copies:
            c.wait()


def direct(spaces, times, precip):
    days, lat, lon = precip.shape
    parts = parts_of(lat)
    early = parts[0][1]
    late = lat + sum(size for _, size in parts[1:])
    block = lon // spaces
    rows = jnp.transpose(precip, (1, 0, 2))
    dma, plain_sem = pltpu.SemaphoreType.DMA, pltpu.SemaphoreType.REGULAR
    vmem, hbm = pl.BlockSpec(memory_space=pltpu.VMEM), pl.BlockSpec(memory_space=pltpu.HBM)

    def shaped(*shape):
        return jax.ShapeDtypeStruct(shape, jnp.float32)

    first, blocks = pl.pallas_call(
        functools.partial(most, spaces, times, early),
        out_shape=(shaped(lat * spaces, block, days), shaped(2, lat, days, block)),
        in_specs=[hbm],
        out_specs=(vmem, vmem),
        scratch_shapes=[
            pltpu.VMEM((lat, days, lon), jnp.float32),
            pltpu.VMEM((spaces - 1, lat, days, block), jnp.float32),
            pltpu.VMEM((lat, 1, lon), jnp.float32),
            pltpu.VMEM((times - 1, lat, 1, lon), jnp.float32),
            pltpu.VMEM((days, days), jnp.float32),
            dma((3,)),
            dma,
            dma((spaces - 1,)),
            dma,
            dma((2,)),
            dma((spaces - 1,)),
            dma,
            dma((times - 1,)),
            plain_sem,
            plain_sem,
            plain_sem,
        ],
        compiler_params=pltpu.CompilerParams(
            collective_id=0, has_side_effects=True, vmem_limit_bytes=GRANT
        ),
        name="most",
    )(rows)
    whole, token = pl.pallas_call(
        put_away,
        out_shape=(shaped(lat * spaces, block, days), shaped(8, 128)),
        in_specs=[vmem],
        out_specs=(hbm, vmem),
        scratch_shapes=[dma],
        compiler_params=pltpu.CompilerParams(vmem_limit_bytes=GRANT),
        name="put_away",
    )(first)
    more = pl.pallas_call(
        functools.partial(rest, spaces, lat, parts),
        out_shape=shaped(late, block, days),
        in_specs=[vmem, vmem],
        out_specs=vmem,
        scratch_shapes=[
            pltpu.VMEM((late, days, block), jnp.float32),
            pltpu.VMEM((days, days), jnp.float32),
            dma((len(parts),)),
            dma((len(parts),)),
        ],
        compiler_params=pltpu.CompilerParams(
            collective_id=1, has_side_effects=True, vmem_limit_bytes=GRANT
        ),
        name="rest",
    )(token, blocks)
    return pl.pallas_call(
        functools.partial(finish, spaces, lat, parts),
        out_shape=shaped(lat * spaces, block, days),
        in_specs=[hbm, vmem],
        out_specs=hbm,
        input_output_aliases={0: 0},
        scratch_shapes=[dma((2,))],
        compiler_params=pltpu.CompilerParams(vmem_limit_bytes=GRANT),
        name="finish",
    )(whole, more)


def plain(precip):
    days = precip.shape[0]
    position = lax.broadcasted_iota(jnp.int32, (days, days), 0)
    later = lax.broadcasted_iota(jnp.int32, (days, days), 1)
    ones = (position <= later).astype(jnp.float32)
    source = lax.all_to_all(precip, "space", split_axis=2, concat_axis=1, tiled=True)
    pixel_major = jnp.transpose(source, (1, 2, 0))
    running = jnp.dot(
        pixel_major, ones, precision=lax.Precision.HIGHEST, preferred_element_type=jnp.float32
    )
    last = lax.all_gather(running[:, :, -1], "tm")
    place = lax.broadcasted_iota(jnp.int32, last.shape, 0)
    carried = jnp.sum(jnp.where(place < lax.axis_index("tm"), last, 0.0), axis=0)
    return running + carried[:, :, None]


def solution(mesh):
    spaces, times = mesh.shape["space"], mesh.shape["tm"]

    def per_device(precip):
        days, lat, lon = precip.shape
        tiled = lon % (spaces * 128) == 0 and days % 128 == 0
        if tiled and lat % sum(PARTS) == 0 and spaces == SPACES and times > 1 and times % 2 == 0:
            return direct(spaces, times, precip)
        return plain(precip)

    return jax.shard_map(
        per_device,
        mesh=mesh,
        in_specs=(P("tm", "space", None),),
        out_specs=P(None, "space", "tm"),
        check_vma=False,
    )
```

time: 142 us -> 140 us (0.986)
  local copies, waits for them, and re-layouts: 2.71 us -> 0 us
    unnamed x1 -> x0, local copies, waits for them, and re-layouts: 2.71 us -> none
    pallas_call x1 -> x4, Pallas kernels: 139 us -> 140 us  [the longest x1 112 us: direct(): pl.pallas_call(functools.partial(most, spaces, times, early), out_shape=(...]
where the time goes in v2:
time: 140 us
  Pallas kernels  140 us (100%)
    pallas_call x1, Pallas kernels, direct(): pl.pallas_call(functools.partial(most, spaces, times, early), out_shape=(...  112 us
    pallas_call x1, Pallas kernels, direct(): pl.pallas_call(functools.partial(rest, spaces, lat, parts), out_shape=sha...  24.3 us

profile of v2, /device:TPU:9, one launch (start us, length us, event | category | flops | bytes accessed | tf_op | source)
XLA Modules:
  0.0 140.0 jit_solution(8225833525594779558)
XLA Ops:
  0.0 112.0 %most.1 = (f32[48,256,128]{2,1,0:T(8,128)S(1)}, f32[2,6,128,256]{3,2,1,0:T(8,128)S(1)}) custom-call(f32[6,128,2048]{2,1,0:T(8,128)} %bitcast.1), custom_call_target="tpu_custom_call" | custom-call | tf_op jit(solution)/shard_map/most/pallas_call | solution.py:349
  112.0 2.7 %put_away.1 = (f32[48,256,128]{2,1,0:T(8,128)}, f32[8,128]{1,0:T(8,128)S(1)}) custom-call(f32[48,256,128]{2,1,0:T(8,128)S(1)} %get-tuple-element.9.first_ref), custom_call_target="tpu_custom_call" | custom-call | tf_op jit(solution)/shard_map/put_away/pallas_call | solution.py:377
  114.7 24.3 %rest.1.late_ref = f32[9,256,128]{2,1,0:T(8,128)S(1)} custom-call(f32[8,128]{1,0:T(8,128)S(1)} %get-tuple-element.11.token_ref, f32[2,6,128,256]{3,2,1,0:T(8,128)S(1)} %get-tuple-element.12.kept), custom_call_target="tpu_custom_call" | custom-call | tf_op jit(solution)/shard_map/rest/pallas_call | solution.py:386
  139.0 1.1 finish.1

commit v3 on v2

--- a/solution.py
+++ b/solution.py
@@ -12,10 +12,10 @@
 ROW = 2
 SPLIT, LAST = 6, 7
 STEPS = {
-    (True, 0): ((), (5, 4, 2, 3), (), (1,), (2, 3, 1, 5, 4)),
-    (True, 1): ((), (2, 3), (), (5, 4, 1), (2, 3, 1, 5, 4)),
-    (False, 0): ((2,), (3,), (1, 5, 4, 7, 6), (), (2, 3, 5, 4, 1, 7, 6)),
-    (False, 1): ((2,), (3,), (1, 7, 6, 5, 4), (), (2, 3, 1, 5, 4, 7, 6)),
+    (True, 0): ((2,), (4, 5, 3), (), (1,), (), (2, 3, 1, 5, 4)),
+    (True, 1): ((), (), (), (5, 4, 2, 1), (3,), (2, 3, 1, 5, 4)),
+    (False, 0): ((2,), (3,), (1, 5, 4, 6, 7), (), (), (2, 3, 5, 4, 1, 6, 7)),
+    (False, 1): ((2,), (3,), (1, 6, 7, 4, 5), (), (), (2, 3, 1, 5, 4, 6, 7)),
 }
 SPACES = 8
 PARTS = (3, 2, 1)
@@ -60,7 +60,7 @@
         pl.when(side & (when % 2 == core))(functools.partial(act, within, core))
 
 
-def most(spaces, times, early, x_ref, out_ref, kept, held, arrived, tot, tots, ones,
+def most(spaces, times, unit, early, x_ref, out_ref, kept, held, arrived, tot, tots, ones,
          load_sem, sent, main_recv, piece_sent, piece_recv, head_recv, tot_send, tot_recv, up, across, go):
     lat, days, lon = x_ref.shape
     block = lon // spaces
@@ -83,8 +83,9 @@
             x_ref.at[span, :, columns(place)], held.at[span, :, columns(place)], load_sem.at[k]
         )
 
-    loads = [load_of(order[0], 0, early, 0), load_of(order[0], early, lat - early, 1)]
-    loads += [load_of(place, 0, lat, 2) for place in order[1:]]
+    cuts = (0, unit, early, lat)
+    loads = [load_of(order[0], at, to - at, k) for k, (at, to) in enumerate(zip(cuts, cuts[1:]))]
+    loads += [load_of(place, 0, lat, len(loads)) for place in order[1:]]
 
     barrier = pltpu.get_barrier_semaphore()
 
@@ -116,9 +117,9 @@
         barrier, jnp.where(z > 0, 1, 0) + jnp.where(z <= low, 1, 0) + jnp.where(z == 0, group, 0)
     )
 
-    def block_copy(step, at_day, size, rows_in, send_sem, recv_sem):
+    def block_copy(step, at_day, size, rows_in, send_sem, recv_sem, at=0):
         peer = flip(me, step, spaces)
-        span, time = pl.ds(0, rows_in), pl.ds(at_day, size)
+        span, time = pl.ds(at, rows_in), pl.ds(at_day, size)
         return pltpu.make_async_remote_copy(
             src_ref=held.at[span, time, columns(peer)],
             dst_ref=arrived.at[step - 1, span, time],
@@ -134,11 +135,12 @@
     def head(step):
         return block_copy(step, 0, HEAD, lat, sent, head_recv.at[step - 1])
 
-    def piece():
-        return block_copy(SPLIT, HEAD, days - HEAD, early, piece_sent, piece_recv.at[0])
+    def piece(k):
+        size = cuts[k + 1] - cuts[k]
+        return block_copy(SPLIT, HEAD, days - HEAD, size, piece_sent, piece_recv.at[k], cuts[k])
 
     def piece_head():
-        return block_copy(SPLIT, 0, HEAD, early, piece_sent, piece_recv.at[1])
+        return block_copy(SPLIT, 0, HEAD, early, piece_sent, piece_recv.at[2])
 
     def total(step):
         return pltpu.make_async_remote_copy(
@@ -157,11 +159,12 @@
 
         by_kind(inner, when, act)
 
-    loads[0].wait()
-
-    @pl.when(inner)
-    def _():
-        piece().start()
+    for k in range(2):
+        loads[k].wait()
+
+        @pl.when(inner)
+        def _():
+            piece(k).start()
 
     @pl.when(z < rows - 1)
     def _():
@@ -178,8 +181,8 @@
         for k in range(1, rows):
             signal(go, space=me + k * ROW)
 
-    loads[1].wait()
-    pltpu.make_async_copy(arrived, arrived, load_sem.at[2]).wait()
+    loads[2].wait()
+    pltpu.make_async_copy(arrived, arrived, load_sem.at[3]).wait()
     send(0)
     for a in range(lat):
         tot[a] = jnp.sum(held[a], axis=0, keepdims=True)
@@ -204,7 +207,7 @@
     def heads(within, core):
         if within:
             piece_head().start()
-        for batch in STEPS[within, core][:4]:
+        for batch in STEPS[within, core][:5]:
             for step in batch:
                 head(step).start()
 
@@ -227,20 +230,24 @@
         out_ref[me * lat + a] = prefix(held[a, :, columns(me)], ones)
 
     def arrivals(within, core):
-        steps = STEPS[within, core][4]
+        steps = STEPS[within, core][5]
         if within:
             main(steps[0]).wait_recv()
             for step in STEPS[within, core][3]:
                 main(step).start()
             piece_head().wait_recv()
-            piece().wait_recv()
+            for k in range(2):
+                piece(k).wait_recv()
             put(flip(me, SPLIT, spaces), SPLIT - 1, early)
         for step in steps:
             head(step).wait_recv()
             if not within or step != steps[0]:
                 main(step).wait_recv()
             put(flip(me, step, spaces), step - 1, lat)
-        count = sum(len(batch) for batch in STEPS[within, core][:4])
+            if step == steps[0]:
+                for other in STEPS[within, core][4]:
+                    main(other).start()
+        count = sum(len(batch) for batch in STEPS[within, core][:5])
         blocks = arrived.at[pl.ds(0, count)]
         pltpu.make_async_copy(blocks, blocks, sent).wait()
         if within:
@@ -258,7 +265,7 @@
     copy.wait()
 
 
-def rest(spaces, lat, parts, token_ref, kept, out_ref, got, ones, sent, received):
+def rest(spaces, lat, parts, token_ref, kept, out_ref, raw, got, ones, sent, received):
     days, block = got.shape[1:]
     me = lax.axis_index("space")
     z = me // ROW
@@ -274,11 +281,11 @@
         upper(ones)
         pl.semaphore_wait(barrier, 2)
 
-    def copy(step, at, size, to, send_sem, recv_sem):
+    def copy(step, at, size, to, send_sem, recv_sem, into=got):
         peer = flip(me, step, spaces)
         return pltpu.make_async_remote_copy(
             src_ref=kept.at[(LAST, SPLIT).index(step), pl.ds(at, size)],
-            dst_ref=got.at[pl.ds(to, size)],
+            dst_ref=into.at[pl.ds(to, size)],
             send_sem=send_sem,
             recv_sem=recv_sem,
             device_id={"space": peer},
@@ -287,9 +294,11 @@
 
     whole = copy(LAST, 0, lat, 0, sent.at[0], received.at[0])
     at, pieces = lat, []
-    for k, (start, size) in enumerate(parts[1:]):
+    for k, (start, size) in enumerate(parts[1:-1]):
         pieces.append((at, size, copy(SPLIT, start, size, at, sent.at[1 + k], received.at[1 + k])))
         at += size
+    k = len(parts) - 1
+    final = copy(SPLIT, *parts[-1], 0, sent.at[k], received.at[k], raw)
 
     def put(at, size):
         @pl.loop(at, at + size)
@@ -301,6 +310,7 @@
         whole.start()
         for _, _, piece in pieces:
             piece.start()
+        final.start()
         whole.wait_recv()
         put(0, lat)
         for k, (at, size, piece) in enumerate(pieces):
@@ -309,26 +319,31 @@
         whole.wait_send()
         for _, _, piece in pieces:
             piece.wait_send()
-
-
-def finish(spaces, lat, parts, all_ref, late_ref, out_ref, sem):
+        final.wait()
+
+
+def finish(spaces, lat, parts, all_ref, late_ref, raw_ref, out_ref, done, ones, sem):
     me = lax.axis_index("space")
     z = me // ROW
     inner = (z == spaces // ROW // 2 - 1) | (z == spaces // ROW // 2)
-    start = parts[1][0]
-
-    def copy(step, at, to, size, k):
+    start, end, last = parts[1][0], *parts[-1]
+
+    def copy(from_ref, step, at, to, size, k):
+        place = flip(me, step, spaces) * lat + to
         return pltpu.make_async_copy(
-            late_ref.at[pl.ds(at, size)],
-            out_ref.at[pl.ds(flip(me, step, spaces) * lat + to, size)],
-            sem.at[k],
+            from_ref.at[pl.ds(at, size)], out_ref.at[pl.ds(place, size)], sem.at[k]
         )
 
     @pl.when(inner)
     def _():
-        copies = [copy(LAST, 0, 0, lat, 0), copy(SPLIT, lat, start, lat - start, 1)]
+        copies = [copy(late_ref, LAST, 0, 0, lat, 0), copy(late_ref, SPLIT, lat, start, end - start, 1)]
         for c in copies:
             c.start()
+        upper(ones)
+        for a in range(last):
+            done[a] = prefix(raw_ref[a], ones)
+        copies.append(copy(done, SPLIT, 0, end, last, 2))
+        copies[-1].start()
         for c in copies:
             c.wait()
 
@@ -337,7 +352,8 @@
     days, lat, lon = precip.shape
     parts = parts_of(lat)
     early = parts[0][1]
-    late = lat + sum(size for _, size in parts[1:])
+    late = lat + sum(size for _, size in parts[1:-1])
+    last = parts[-1][1]
     block = lon // spaces
     rows = jnp.transpose(precip, (1, 0, 2))
     dma, plain_sem = pltpu.SemaphoreType.DMA, pltpu.SemaphoreType.REGULAR
@@ -347,7 +363,7 @@
         return jax.ShapeDtypeStruct(shape, jnp.float32)
 
     first, blocks = pl.pallas_call(
-        functools.partial(most, spaces, times, early),
+        functools.partial(most, spaces, times, lat // sum(PARTS), early),
         out_shape=(shaped(lat * spaces, block, days), shaped(2, lat, days, block)),
         in_specs=[hbm],
         out_specs=(vmem, vmem),
@@ -357,11 +373,11 @@
             pltpu.VMEM((lat, 1, lon), jnp.float32),
             pltpu.VMEM((times - 1, lat, 1, lon), jnp.float32),
             pltpu.VMEM((days, days), jnp.float32),
-            dma((3,)),
+            dma((4,)),
             dma,
             dma((spaces - 1,)),
             dma,
-            dma((2,)),
+            dma((3,)),
             dma((spaces - 1,)),
             dma,
             dma((times - 1,)),
@@ -383,11 +399,11 @@
         compiler_params=pltpu.CompilerParams(vmem_limit_bytes=GRANT),
         name="put_away",
     )(first)
-    more = pl.pallas_call(
+    more, raw = pl.pallas_call(
         functools.partial(rest, spaces, lat, parts),
-        out_shape=shaped(late, block, days),
+        out_shape=(shaped(late, block, days), shaped(last, days, block)),
         in_specs=[vmem, vmem],
-        out_specs=vmem,
+        out_specs=(vmem, vmem),
         scratch_shapes=[
             pltpu.VMEM((late, days, block), jnp.float32),
             pltpu.VMEM((days, days), jnp.float32),
@@ -402,13 +418,17 @@
     return pl.pallas_call(
         functools.partial(finish, spaces, lat, parts),
         out_shape=shaped(lat * spaces, block, days),
-        in_specs=[hbm, vmem],
+        in_specs=[hbm, vmem, vmem],
         out_specs=hbm,
         input_output_aliases={0: 0},
-        scratch_shapes=[dma((2,))],
+        scratch_shapes=[
+            pltpu.VMEM((last, block, days), jnp.float32),
+            pltpu.VMEM((days, days), jnp.float32),
+            dma((3,)),
+        ],
         compiler_params=pltpu.CompilerParams(vmem_limit_bytes=GRANT),
         name="finish",
-    )(whole, more)
+    )(whole, more, raw)
 
 
 def plain(precip):

time: 140 us -> 140 us (level)
  no operation moved by 1% of the time
where the time goes in v3:
time: 140 us
  Pallas kernels  140 us (100%)
    pallas_call x1, Pallas kernels, direct(): pl.pallas_call(functools.partial(most, spaces, times, lat // sum(PARTS),...  114 us
    pallas_call x1, Pallas kernels, direct(): pl.pallas_call(functools.partial(rest, spaces, lat, parts), out_shape=(sh...  22.4 us

profile of v3, /device:TPU:9, one launch (start us, length us, event | category | flops | bytes accessed | tf_op | source)
XLA Modules:
  0.0 139.8 jit_solution(10048879922388593341)
XLA Ops:
  0.0 113.6 %most.1 = (f32[48,256,128]{2,1,0:T(8,128)S(1)}, f32[2,6,128,256]{3,2,1,0:T(8,128)S(1)}) custom-call(f32[6,128,2048]{2,1,0:T(8,128)} %bitcast.1), custom_call_target="tpu_custom_call" | custom-call | tf_op jit(solution)/shard_map/most/pallas_call | solution.py:365
  113.6 2.7 %put_away.1 = (f32[48,256,128]{2,1,0:T(8,128)}, f32[8,128]{1,0:T(8,128)S(1)}) custom-call(f32[48,256,128]{2,1,0:T(8,128)S(1)} %get-tuple-element.11.first_ref), custom_call_target="tpu_custom_call" | custom-call | tf_op jit(solution)/shard_map/put_away/pallas_call | solution.py:393
  116.3 22.4 %rest.1 = (f32[8,256,128]{2,1,0:T(8,128)S(1)}, f32[1,128,256]{2,1,0:T(8,128)S(1)}) custom-call(f32[8,128]{1,0:T(8,128)S(1)} %get-tuple-element.13.token_ref, f32[2,6,128,256]{3,2,1,0:T(8,128)S(1)} %get-tuple-element.14.kept), custom_call_target="tpu_custom_call" | custom-call | tf_op jit(solution)/shard_map/rest/pallas_call | solution.py:402
  138.7 1.1 finish.1

commit v4 on v3

--- a/solution.py
+++ b/solution.py
@@ -12,10 +12,10 @@
 ROW = 2
 SPLIT, LAST = 6, 7
 STEPS = {
-    (True, 0): ((2,), (4, 5, 3), (), (1,), (), (2, 3, 1, 5, 4)),
+    (True, 0): ((4, 2), (5,), (), (3, 1), (), (2, 3, 1, 5, 4)),
     (True, 1): ((), (), (), (5, 4, 2, 1), (3,), (2, 3, 1, 5, 4)),
-    (False, 0): ((2,), (3,), (1, 5, 4, 6, 7), (), (), (2, 3, 5, 4, 1, 6, 7)),
-    (False, 1): ((2,), (3,), (1, 6, 7, 4, 5), (), (), (2, 3, 1, 5, 4, 6, 7)),
+    (False, 0): ((2,), (3,), (5, 4, 6, 7), (), (1,), (2, 3, 5, 4, 6, 7, 1)),
+    (False, 1): ((2,), (3,), (6, 7, 4, 5), (), (1,), (2, 3, 5, 4, 6, 7, 1)),
 }
 SPACES = 8
 PARTS = (3, 2, 1)
@@ -61,7 +61,7 @@
 
 
 def most(spaces, times, unit, early, x_ref, out_ref, kept, held, arrived, tot, tots, ones,
-         load_sem, sent, main_recv, piece_sent, piece_recv, head_recv, tot_send, tot_recv, up, across, go):
+         load_sem, sent, main_recv, piece_sent, piece_recv, head_recv, tot_send, tot_recv, up, down, across, go):
     lat, days, lon = x_ref.shape
     block = lon // spaces
     rows = spaces // ROW
@@ -159,6 +159,10 @@
 
         by_kind(inner, when, act)
 
+    @pl.when(z == low)
+    def _():
+        signal(down, space=me + ROW)
+
     for k in range(2):
         loads[k].wait()
 
@@ -173,6 +177,10 @@
     @pl.when(z > 0)
     def _():
         signal(up, space=me - ROW)
+
+    @pl.when(z == high)
+    def _():
+        pl.semaphore_wait(down, 1)
 
     @pl.when(z == 0)
     def _():
@@ -381,6 +389,7 @@
             dma((spaces - 1,)),
             dma,
             dma((times - 1,)),
+            plain_sem,
             plain_sem,
             plain_sem,
             plain_sem,

time: 140 us -> 139 us (level)
  no operation moved by 1% of the time
where the time goes in v4:
time: 139 us
  Pallas kernels  139 us (100%)
    pallas_call x1, Pallas kernels, direct(): pl.pallas_call(functools.partial(most, spaces, times, lat // sum(PARTS),...  113 us
    pallas_call x1, Pallas kernels, direct(): pl.pallas_call(functools.partial(rest, spaces, lat, parts), out_shape=(sh...  22.4 us

profile of v4, /device:TPU:9, one launch (start us, length us, event | category | flops | bytes accessed | tf_op | source)
XLA Modules:
  0.0 139.2 jit_solution(6222244587081769356)
XLA Ops:
  0.0 113.0 %most.1 = (f32[48,256,128]{2,1,0:T(8,128)S(1)}, f32[2,6,128,256]{3,2,1,0:T(8,128)S(1)}) custom-call(f32[6,128,2048]{2,1,0:T(8,128)} %bitcast.1), custom_call_target="tpu_custom_call" | custom-call | tf_op jit(solution)/shard_map/most/pallas_call | solution.py:373
  113.0 2.7 %put_away.1 = (f32[48,256,128]{2,1,0:T(8,128)}, f32[8,128]{1,0:T(8,128)S(1)}) custom-call(f32[48,256,128]{2,1,0:T(8,128)S(1)} %get-tuple-element.11.first_ref), custom_call_target="tpu_custom_call" | custom-call | tf_op jit(solution)/shard_map/put_away/pallas_call | solution.py:402
  115.7 22.4 %rest.1 = (f32[8,256,128]{2,1,0:T(8,128)S(1)}, f32[1,128,256]{2,1,0:T(8,128)S(1)}) custom-call(f32[8,128]{1,0:T(8,128)S(1)} %get-tuple-element.13.token_ref, f32[2,6,128,256]{3,2,1,0:T(8,128)S(1)} %get-tuple-element.14.kept), custom_call_target="tpu_custom_call" | custom-call | tf_op jit(solution)/shard_map/rest/pallas_call | solution.py:411
  138.1 1.1 finish.1
